TPU v7x, 32 devices: a whole 2x2x4 slice. The times are simulated.
32 devices in a mesh: grp: 4 (over y, core), mem: 8 (over z, x).
Axes of the slice: x: 2, y: 2, z: 4, core: 2. Of those that a mesh axis runs over, the one named last changes fastest.
Arguments:
- factors: bfloat16 [64, 288, 1792], P(('grp', 'mem')), may hold values from -1.5 to 1.5
- screen: int32 [32, 18], P(('grp', 'mem')), may hold values from 0 to 1, as said below
Outputs:
- exchange_matrix: float32 [1792, 1792], P(('grp', 'mem'))
Inputs may be any that keep to these rules, and one draw needn't show every extreme that they name: screen[b, j] is 1 where auxiliary block b and occupied block j survive screening; every auxiliary block keeps at least one occupied block.
All inputs are finite; a program needn't handle non-finite values.
Results may differ from a plain program's by a relative error of at most 0.0003.
Values may be sent and summed in bfloat16 or wider, within the bound.
A program may use at most 128 MiB of HBM per device.

v0:
```python
import functools

import jax
import jax.numpy as jnp
from jax import lax
from jax.experimental import pallas as pl
from jax.experimental.pallas import tpu as pltpu
from jax.sharding import PartitionSpec as P

LANES = 128
TOP = 32767.0
KINDS = "DGCFGFG"
STEPS = [0, 1, 2, 3, 4, 0, 1, 5, 6, 2, 3, 4, 0, 1, 5, 6]
MESH = pl.DeviceIdType.MESH


def bits_of(size):
    return size.bit_length() - 1


def plan_for(groups, members, parts):
    near = [[("mem", 1)]]
    rows = [[("grp", 2 << k)] for k in range(bits_of(groups) - 1)]
    far = [("mem", 2 << k) for k in range(bits_of(members) - 1)]
    single = [[bit] for bit in far]
    direct = [far[k : k + 2][::-1] for k in range(0, len(far), 2)]
    kinds = {
        "A": near + rows + direct,
        "B": rows + near + direct,
        "C": single + near + rows,
        "D": near + single + rows,
        "E": rows + single + near,
        "F": near + rows + single,
        "G": rows + near + single,
    }
    return [kinds[KINDS[p % len(KINDS)]] for p in range(parts)]


def messages_of(stages):
    left = 1
    for bits in stages:
        left <<= len(bits)
    result, slot = [], 0
    for level, bits in enumerate(stages):
        left >>= len(bits)
        for target in range(1, 1 << len(bits)):
            result.append((level, target, target * left, left, slot))
            slot += left
    return result


def kernel(
    groups, members, plan, chunks, width, x_ref, screen_ref, out_ref,
    both, turned, total, sent, got, sent_top, got_top, last,
    pair_send, pair_recv, data_send, data_recv, top_send, top_recv, end_send, end_recv,
):
    depth, basis = x_ref.shape
    own_rows = out_ref.shape[0]
    half = basis // 2
    occ_blocks = screen_ref.shape[1]
    grp, mem = lax.axis_index("grp"), lax.axis_index("mem")
    core = lax.rem(grp, 2)
    place = {"grp": grp, "mem": mem}
    def peer(bits):
        there = dict(place)
        for axis, step in bits:
            bit = lax.rem(place[axis] // step, 2)
            there[axis] = there[axis] + (1 - 2 * bit) * step
        return there["grp"], there["mem"]

    def chosen(bits, target):
        return tuple(b for t, b in enumerate(bits) if target >> (len(bits) - 1 - t) & 1)

    partner = peer([("grp", 1)])
    barrier = pltpu.get_barrier_semaphore()
    met = {
        tuple(sorted(chosen(stages[level], target)))
        for stages in plan
        for level, target, *_ in messages_of(stages)
    }
    peers = [partner] + [peer(bits) for bits in sorted(met)]
    for other in peers:
        pl.semaphore_signal(barrier, inc=1, device_id=other, device_id_type=MESH)


    def mask(j, carry):
        at = pl.ds(pl.multiple_of(j * width, width), width)
        keep = screen_ref[0, lax.rem(j, occ_blocks)].astype(jnp.float32)
        both[at, :] = (x_ref[at, :].astype(jnp.float32) * keep).astype(both.dtype)
        return carry

    pieces = 2
    piece = depth // pieces
    pair = []
    for n in range(pieces):
        lax.fori_loop(n * piece // width, (n + 1) * piece // width, mask, 0)
        if n == 0:
            pl.semaphore_wait(barrier, len(peers))
        pair.append(
            pltpu.make_async_remote_copy(
                src_ref=both.at[pl.ds(n * piece, piece)],
                dst_ref=both.at[pl.ds(depth + n * piece, piece)],
                send_sem=pair_send.at[n], recv_sem=pair_recv.at[n],
                device_id=partner, device_id_type=MESH,
            )
        )
        pair[-1].start()

    def turn(low, high):
        def one(m, carry):
            at = pl.ds(pl.multiple_of(m * 256, 256), 256)
            for k in range(low, high, LANES):
                turned[at, k : k + LANES] = both[k : k + LANES, at].T
            return carry

        lax.fori_loop(0, basis // 256, one, 0)

    early = depth // LANES * LANES
    turn(0, early)
    for copy in pair:
        copy.wait_recv()
    turn(early, 2 * depth)

    def rows_at(stages, index):
        order = [bit for bits in stages for bit in bits]
        at = {"grp": grp - core, "mem": mem}
        for t, (axis, step) in enumerate(order):
            flip = index // (1 << (len(order) - 1 - t)) % 2
            bit = lax.rem(place[axis] // step, 2)
            at[axis] = at[axis] + flip * (1 - 2 * bit) * step
        first = (at["grp"] * members + at["mem"]) * own_rows
        second = first + members * own_rows
        return [pl.ds(pl.multiple_of(r, 8), own_rows) for r in (first, second)]

    def repeat(low, high, body):
        count = high - low
        by = 4 if count % 4 == 0 else count

        def step(t, carry):
            for u in range(by):
                body(low + t * by + u)
            return carry

        if count == by:
            step(0, 0)
        else:
            lax.fori_loop(0, count // by, step, 0)

    def columns(p):
        return slice(p * LANES, (p + 1) * LANES)

    def current(p, index, order):
        return jnp.concatenate([total[r, columns(p)] for r in rows_at(order, index)], axis=0)

    def arrived(p, level, index):
        value = None
        for m, (at, _, _, _, slot) in enumerate(messages_of(plan[p])):
            if at == level:
                top = got_top[p, m, pl.ds(index, 1), :] * (1.0 / TOP)
                one = got[p, slot + index].astype(jnp.int32).astype(jnp.float32) * top
                value = one if value is None else value + one
        return value

    def copies(p, m):
        level, target, _, count, slot = messages_of(plan[p])[m]
        run = pl.ds(slot, count)
        to = peer(chosen(plan[p][level], target))
        return [
            pltpu.make_async_remote_copy(
                src_ref=here, dst_ref=there, send_sem=a.at[p, m], recv_sem=b.at[p, m],
                device_id=to, device_id_type=MESH,
            )
            for here, there, a, b in (
                (sent.at[p, run], got.at[p, run], data_send, data_recv),
                (sent_top.at[p, m], got_top.at[p, m], top_send, top_recv),
            )
        ]

    def send(p, level):
        for m, (at, _, first, count, slot) in reversed(list(enumerate(messages_of(plan[p])))):
            if at != level:
                continue

            def pack(i):
                value = current(p, first + i, plan[p])
                if level:
                    value = value + arrived(p, level - 1, first + i)
                top = jnp.max(jnp.abs(value), axis=0, keepdims=True)
                scale = TOP / jnp.maximum(top, 2e-34)
                sent[p, slot + i] = jnp.round(value * scale).astype(jnp.int32).astype(jnp.int16)
                sent_top[p, m, pl.ds(i, 1), :] = top

            repeat(0, count, pack)
            for copy in copies(p, m):
                copy.start()

    def wait(p, level):
        for m, (at, *_) in enumerate(messages_of(plan[p])):
            if at == level:
                for copy in copies(p, m):
                    copy.wait_recv()

    def keep(p, level):
        count = [n for at, _, _, n, _ in messages_of(plan[p]) if at == level][0]
        if level + 1 < len(plan[p]):
            count >>= len(plan[p][level + 1])

        def add(i):
            value = arrived(p, level, i)
            for n, r in enumerate(rows_at(plan[p], i)):
                total[r, columns(p)] += value[n * own_rows : (n + 1) * own_rows]

        repeat(0, count, add)

    parts = len(plan)
    mine = pl.ds(pl.multiple_of((grp * members + mem) * own_rows, 8), own_rows)
    theirs = pl.ds(pl.multiple_of((partner[0] * members + mem) * own_rows, 8), own_rows)
    ends = []

    def advance(p, level):
        wait(p, level)
        if level + 1 < len(plan[p]):
            send(p, level + 1)
            keep(p, level)
            return
        keep(p, level)
        last[p] = total[theirs, columns(p)]
        at = pl.ds(pl.multiple_of(core * half + p * LANES, LANES), LANES)
        copy = pltpu.make_async_remote_copy(
            src_ref=last.at[p], dst_ref=out_ref.at[:, at],
            send_sem=end_send.at[p], recv_sem=end_recv.at[p],
            device_id=partner, device_id_type=MESH,
        )
        copy.start()
        ends.append(copy)
        out_ref[:, at] = total[mine, columns(p)]

    def multiply(low, high):
        def one(m, carry):
            tall = basis // 2
            at = pl.ds(pl.multiple_of(m * tall, LANES), tall)
            total[at, low:high] = jnp.dot(
                turned[at, :],
                both[:, pl.ds(pl.multiple_of(core * half + low, LANES), high - low)],
                preferred_element_type=jnp.float32,
            )
            return carry

        lax.fori_loop(0, 2, one, 0)

    step = [0] * parts
    made = 0
    for p in STEPS + list(range(parts)) * (2 + max(len(stages) for stages in plan)):
        if p >= parts or step[p] > len(plan[p]):
            continue
        if step[p] == 0:
            while chunks[made][0] <= p * LANES if made < len(chunks) else False:
                multiply(*chunks[made])
                made += 1
            send(p, 0)
        else:
            advance(p, step[p] - 1)
        step[p] += 1
    for copy in pair:
        copy.wait_send()
    for p in range(parts):
        for m in range(len(messages_of(plan[p]))):
            for copy in copies(p, m):
                copy.wait_send()
    for copy in ends:
        copy.wait()


def solution(mesh):
    groups, members = mesh.shape["grp"], mesh.shape["mem"]

    def on_device(factors, screen):
        aux_rows, occ_count, basis = factors.shape
        depth = aux_rows * occ_count
        devices = groups * members
        real_rows = basis // devices
        own_rows = (real_rows + 7) // 8 * 8
        rows = factors.reshape(depth, basis)
        if own_rows != real_rows:
            rows = rows.reshape(depth, devices, real_rows)
            rows = jnp.pad(rows, ((0, 0), (0, 0), (0, own_rows - real_rows)))
            basis = devices * own_rows
            rows = rows.reshape(depth, basis)
        half = basis // 2
        parts = half // LANES
        plan = plan_for(groups, members, parts)
        chunks = [(low, min(low + 2 * LANES, half)) for low in range(0, half, 2 * LANES)]
        chips = groups * members // 2
        levels = max(len(messages_of(stages)) for stages in plan)
        block = 2 * own_rows
        places = max(8, chips // 2)
        dma = pltpu.SemaphoreType.DMA
        vmem = pl.BlockSpec(memory_space=pltpu.VMEM)
        result = pl.pallas_call(
            functools.partial(kernel, groups, members, plan, chunks, occ_count // screen.shape[1]),
            out_shape=pltpu.VMEM((own_rows, basis), jnp.float32),
            in_specs=[vmem, pl.BlockSpec(memory_space=pltpu.SMEM)],
            out_specs=vmem,
            scratch_shapes=[
                pltpu.VMEM((2 * depth, basis), jnp.bfloat16),
                pltpu.VMEM((basis, 2 * depth), jnp.bfloat16),
                pltpu.VMEM((basis, half), jnp.float32),
                pltpu.VMEM((parts, chips - 1, block, LANES), jnp.int16),
                pltpu.VMEM((parts, chips - 1, block, LANES), jnp.int16),
                pltpu.VMEM((parts, levels, places, LANES), jnp.float32),
                pltpu.VMEM((parts, levels, places, LANES), jnp.float32),
                pltpu.VMEM((parts, own_rows, LANES), jnp.float32),
                dma((2,)), dma((2,)),
                dma((parts, levels)), dma((parts, levels)),
                dma((parts, levels)), dma((parts, levels)),
                dma((parts,)), dma((parts,)),
            ],
            compiler_params=pltpu.CompilerParams(
                collective_id=0, has_side_effects=True, vmem_limit_bytes=60 * 1024 * 1024
            ),
        )(rows, screen)
        if own_rows != real_rows:
            result = result[:real_rows].reshape(real_rows, devices, own_rows)[:, :, :real_rows]
            result = result.reshape(real_rows, devices * real_rows)
        return result

    placed = (P(("grp", "mem"), None, None), P(("grp", "mem"), None))
    return jax.shard_map(
        on_device, mesh=mesh, in_specs=placed, out_specs=P(("grp", "mem"), None), check_vma=False
    )
```

profile of v0, /device:TPU:0, one launch (start us, length us, event | category | flops | bytes accessed | tf_op | source)
XLA Modules:
  0.0 49.4 jit_solution(14540535207378269747)
XLA Ops:
  0.0 48.6 %shard_map.28 = f32[56,1792]{1,0:T(8,128)S(1)} custom-call(bf16[576,1792]{1,0:T(8,128)(2,1)} %bitcast.1, s32[1,18]{1,0:T(1,128)} %screen_ref.1), custom_call_target="tpu_custom_call" | custom-call | tf_op jit(solution)/shard_map/pallas_call | solution.py:299
  48.6 0.8 %copy.4 = f32[56,1792]{1,0:T(8,128)} copy(f32[56,1792]{1,0:T(8,128)S(1)} %shard_map.28) | data formatting | bytes 802816
where the time goes:
time: 49.5 us; the launch traced here: 49.4 us
  Pallas kernels  48.6 us (98%)
  local copies, waits for them, and re-layouts  0.75 us (2%)
    pallas_call x1, Pallas kernels, on_device(): pl.pallas_call(functools.partial(kernel, groups, members, plan, chunks, o...  48.6 us

commit v1 on v0

--- a/solution.py
+++ b/solution.py
@@ -271,6 +271,485 @@
         copy.wait()
 
 
+NEAR, ROW = ("mem", 1), ("grp", 2)
+ORDERS = ["xyab", "ayxb", "yabx", "yxab"]
+STEPS_AFTER = [0, 0, 2, 1, 3, 2, 0, 1, 3, 2, 0, 1, 3, 2, 1, 3]
+
+
+def circle_plan(groups, members, parts):
+    far = [("mem", 2 << k) for k in range(bits_of(members) - 1)]
+    letters = {
+        "x": [[NEAR]],
+        "y": [[("grp", 2 << k)] for k in range(bits_of(groups) - 1)],
+        "a": [far[:1]],
+        "b": [[bit] for bit in far[1:]],
+        "z": [far[::-1]],
+    }
+    orders = [ORDERS[p % len(ORDERS)] for p in range(parts)]
+    return [[stage for letter in order for stage in letters[letter]] for order in orders]
+
+
+def place_of(groups, members, at):
+    ladder, line = groups // 2, members // 2
+    w, z = at // line, at % line
+    z = line - 1 - z if w % 2 else z
+    return (w, z, 0) if w < ladder else (2 * ladder - 1 - w, z, 1)
+
+
+def moves_of(groups, members, own_rows, basis):
+    unit = 2 * own_rows
+    moves = []
+    for low in range(0, basis, LANES):
+        pieces, c = [], low
+        while c < low + LANES:
+            y, z, x = place_of(groups, members, c // unit)
+            half, off = c % unit // own_rows, c % own_rows
+            source = ((2 * y + half) * members + 2 * z + x) * own_rows + off
+            count = min(own_rows - off, low + LANES - c, LANES - source % LANES)
+            pieces.append((c - low, source // LANES, (c - low - source) % LANES))
+            c += count
+        moves.append(pieces)
+    return moves
+
+
+def circle_kernel(
+    groups, members, plan, width, x_hbm, screen_ref, out_ref,
+    x_ref, both, turned, total, sent, got, sent_top, got_top, last, window, flipped, around,
+    load, pair_send, pair_recv, data_send, data_recv, top_send, top_recv, end_send, end_recv,
+    flip_send, flip_recv,
+):
+    depth, basis = x_ref.shape
+    own_rows = out_ref.shape[0]
+    pieces = pair_send.shape[0]
+    piece = depth // pieces
+    loads = []
+    for n in range(pieces):
+        at = pl.ds(n * piece, piece)
+        loads.append(pltpu.make_async_copy(x_hbm.at[at], x_ref.at[at], load.at[n]))
+        loads[-1].start()
+    unit = 2 * own_rows
+    chips = groups * members // 2
+    line, ladder = members // 2, groups // 2
+    reach = chips // 2
+    parts = len(plan)
+    panels = basis // LANES
+    occ_blocks = screen_ref.shape[1]
+    grp, mem = lax.axis_index("grp"), lax.axis_index("mem")
+    core = lax.rem(grp, 2)
+    place = {"grp": grp - core, "mem": mem}
+    lane = lax.broadcasted_iota(jnp.int32, (1, LANES), 1)
+    swap = {NEAR: ROW, ROW: NEAR}
+
+    def step_of(bit):
+        axis, step = bit
+        return step * (1 - 2 * lax.rem(place[axis] // step, 2))
+
+    def moved(bits):
+        there = dict(place)
+        for bit in bits:
+            other = swap.get(bit, bit)
+            if other == bit:
+                there[bit[0]] = there[bit[0]] + step_of(bit)
+            else:
+                there[bit[0]] = there[bit[0]] + step_of(bit) * (1 - core)
+                there[other[0]] = there[other[0]] + step_of(other) * core
+        return there["grp"], there["mem"]
+
+    def peer(bits):
+        g, m = moved(bits)
+        return g + core, m
+
+    def spot(g, m):
+        y, z, x = g // 2, m // 2, lax.rem(m, 2)
+        w = jnp.where(x == 1, 2 * ladder - 1 - y, y)
+        return w * line + jnp.where(lax.rem(w, 2) == 1, line - 1 - z, z)
+
+    def holder(at):
+        w, z = at // line, lax.rem(at, line)
+        z = jnp.where(lax.rem(w, 2) == 1, line - 1 - z, z)
+        x = jnp.where(w >= ladder, 1, 0)
+        y = jnp.where(w >= ladder, 2 * ladder - 1 - w, w)
+        return 2 * y, 2 * z + x
+
+    def chosen(bits, target):
+        return tuple(b for t, b in enumerate(bits) if target >> (len(bits) - 1 - t) & 1)
+
+    own = spot(grp, mem)
+    partner = (grp + 1 - 2 * core, mem)
+    barrier = pltpu.get_barrier_semaphore()
+    met = {
+        tuple(sorted(chosen(stages[level], target)))
+        for stages in plan
+        for level, target, *_ in messages_of(stages)
+    }
+    met |= {tuple(sorted(swap.get(b, b) for b in bits)) for bits in met}
+    peers = [partner] + [peer(bits) for bits in sorted(met)]
+    for other in peers:
+        pl.semaphore_signal(barrier, inc=1, device_id=other, device_id_type=MESH)
+
+    moves = moves_of(groups, members, own_rows, basis)
+
+    def arrange(j, carry):
+        for u in range(strips):
+            row = j * strips + u
+            at = pl.ds(pl.multiple_of(row * width, width), width)
+            keep = screen_ref[0, lax.rem(row, occ_blocks)].astype(jnp.float32).astype(both.dtype)
+            for n, pieces in enumerate(moves):
+                value = None
+                for first, m, shift in pieces:
+                    piece = x_ref[at, columns(m)]
+                    piece = pltpu.roll(piece, shift, 1) if shift else piece
+                    value = piece if value is None else jnp.where(lane >= first, piece, value)
+                value = value * keep
+                both[at, columns(n)] = value
+                if n == 0:
+                    both[at, columns(panels)] = value
+        return carry
+
+    def columns(p):
+        return slice(p * LANES, (p + 1) * LANES)
+
+    strips = 3
+    pair = []
+    for n in range(pieces):
+        with jax.named_scope(f"load{n}"):
+            loads[n].wait()
+        with jax.named_scope(f"arrange{n}"):
+            count = piece // width // strips
+            lax.fori_loop(n * count, (n + 1) * count, arrange, 0)
+        if n == 0:
+            with jax.named_scope("barrier"):
+                pl.semaphore_wait(barrier, len(peers))
+        pair.append(
+            pltpu.make_async_remote_copy(
+                src_ref=both.at[pl.ds(n * piece, piece)],
+                dst_ref=both.at[pl.ds(depth + n * piece, piece)],
+                send_sem=pair_send.at[n], recv_sem=pair_recv.at[n],
+                device_id=partner, device_id_type=MESH,
+            )
+        )
+        pair[-1].start()
+
+    def turn(low, high):
+        def one(m, carry):
+            at = pl.ds(pl.multiple_of(m * wide, LANES), wide)
+            for k in range(low, high, LANES):
+                turned[at, k : k + LANES] = both[k : k + LANES, at].T
+            return carry
+
+        wide = basis // 2
+        lax.fori_loop(0, 2, one, 0)
+
+    early = depth // LANES * LANES
+    with jax.named_scope("turn"):
+        turn(0, early)
+    done = 0
+    for low in range(early, 2 * depth, LANES):
+        while done < pieces and low + LANES > depth + done * piece:
+            with jax.named_scope(f"pair{done}"):
+                pair[done].wait_recv()
+            done += 1
+        with jax.named_scope(f"turn{low}"):
+            turn(low, low + LANES)
+
+    def rows_of(stages, index):
+        order = [bit for bits in stages for bit in bits]
+        flips = [b for t, b in enumerate(order) if False]
+        there = dict(place)
+        for t, bit in enumerate(order):
+            flip = index // (1 << (len(order) - 1 - t)) % 2
+            other = swap.get(bit, bit)
+            if other == bit:
+                there[bit[0]] = there[bit[0]] + flip * step_of(bit)
+            else:
+                there[bit[0]] = there[bit[0]] + flip * step_of(bit) * (1 - core)
+                there[other[0]] = there[other[0]] + flip * step_of(other) * core
+        return spot(there["grp"], there["mem"])
+
+    def repeat(low, high, body):
+        count = high - low
+        by = 8 if count % 8 == 0 else count
+
+        def step(t, carry):
+            for u in range(by):
+                body(low + t * by + u)
+            return carry
+
+        if count == by:
+            step(0, 0)
+        else:
+            lax.fori_loop(0, count // by, step, 0)
+
+    def panel_of(p):
+        return jnp.where(core == 0, parts - 1 - p, parts + p)
+
+    def block_at(s):
+        return pl.ds(pl.multiple_of(s * unit, 16), unit)
+
+    def product(p, s):
+        start = s * unit + panel_of(p) * LANES
+        start = jnp.where(start >= basis, start - basis, start)
+        n = start // LANES
+        a = start - n * LANES
+        value = jnp.dot(
+            turned[block_at(s), :],
+            both[:, pl.ds(pl.multiple_of(n * LANES, LANES), 2 * LANES)],
+            preferred_element_type=jnp.float32,
+        )
+        value = jnp.where(lane >= a, value[:, :LANES], value[:, LANES:])
+        return pltpu.roll(value, jnp.where(a == 0, 0, LANES - a), 1)
+
+    def current(p, index):
+        return total[block_at(rows_of(plan[p], index)), columns(p)]
+
+    def arrived(p, level, index):
+        value = None
+        for m, (at, _, _, _, slot) in enumerate(messages_of(plan[p])):
+            if at == level:
+                top = got_top[p, m, pl.ds(index, 1), :] * (1.0 / TOP)
+                one = got[p, slot + index].astype(jnp.int32).astype(jnp.float32) * top
+                value = one if value is None else value + one
+        return value
+
+    def copies(p, m):
+        level, target, _, count, slot = messages_of(plan[p])[m]
+        run = pl.ds(slot, count)
+        to = peer(chosen(plan[p][level], target))
+        return [
+            pltpu.make_async_remote_copy(
+                src_ref=here, dst_ref=there, send_sem=a.at[p, m], recv_sem=b.at[p, m],
+                device_id=to, device_id_type=MESH,
+            )
+            for here, there, a, b in (
+                (sent.at[p, run], got.at[p, run], data_send, data_recv),
+                (sent_top.at[p, m], got_top.at[p, m], top_send, top_recv),
+            )
+        ]
+
+    def send(p, level):
+        for m, (at, _, first, count, slot) in reversed(list(enumerate(messages_of(plan[p])))):
+            if at != level:
+                continue
+
+            def pack(i):
+                if level:
+                    value = current(p, first + i) + arrived(p, level - 1, first + i)
+                else:
+                    value = product(p, rows_of(plan[p], first + i))
+                top = jnp.max(jnp.abs(value), axis=0, keepdims=True)
+                scale = TOP / jnp.maximum(top, 2e-34)
+                sent[p, slot + i] = jnp.round(value * scale).astype(jnp.int32).astype(jnp.int16)
+                sent_top[p, m, pl.ds(i, 1), :] = top
+
+            repeat(0, count, pack)
+            for copy in copies(p, m):
+                copy.start()
+
+    def remaining(p, level):
+        count = [n for at, _, _, n, _ in messages_of(plan[p]) if at == level][0]
+        return count
+
+    def fill(p):
+        def one(i):
+            s = rows_of(plan[p], i)
+            total[block_at(s), columns(p)] = product(p, s)
+
+        repeat(0, remaining(p, 0), one)
+
+    def wait(p, level):
+        for m, (at, *_) in enumerate(messages_of(plan[p])):
+            if at == level:
+                for copy in copies(p, m):
+                    copy.wait_recv()
+
+    def keep(p, level):
+        count = remaining(p, level)
+        if level + 1 < len(plan[p]):
+            count >>= len(plan[p][level + 1])
+
+        def add(i):
+            total[block_at(rows_of(plan[p], i)), columns(p)] += arrived(p, level, i)
+
+        repeat(0, count, add)
+
+    def cuts(p, side):
+        q = parts - 1 - p if side == 0 else parts + p
+        marks = sorted({q * LANES, (q + 1) * LANES} | {
+            r for r in range(q * LANES, (q + 1) * LANES) if r % own_rows == 0
+        })
+        result = []
+        for t, (low, high) in enumerate(zip(marks, marks[1:])):
+            k, half = low // unit, low % unit // own_rows
+            if 0 < k < reach:
+                result.append((q, t, k, half, low - q * LANES, low % own_rows, high - low))
+        return result
+
+    def flips(p, side):
+        result = []
+        for q, t, k, half, here, there, count in cuts(p, side):
+            g, m = holder(lax.rem(own + k, chips))
+            copy = pltpu.make_async_remote_copy(
+                src_ref=flipped.at[p, pl.ds(here, count)],
+                dst_ref=around.at[chips - k, pl.ds(there, count)],
+                send_sem=flip_send.at[p, t], recv_sem=flip_recv.at[q, t],
+                device_id=(g + half, m), device_id_type=MESH,
+            )
+            result.append((half, copy))
+        return result
+
+    def ends(p):
+        q = panel_of(p)
+        at = pl.ds(pl.multiple_of(q * LANES, LANES), LANES)
+        return pltpu.make_async_remote_copy(
+            src_ref=last.at[p], dst_ref=window.at[:, at],
+            send_sem=end_send.at[p], recv_sem=end_recv.at[p],
+            device_id=partner, device_id_type=MESH,
+        )
+
+    def finish(p):
+        mine = pl.ds(pl.multiple_of(own * unit + core * own_rows, 8), own_rows)
+        theirs = pl.ds(pl.multiple_of(own * unit + (1 - core) * own_rows, 8), own_rows)
+        value = total[block_at(own), columns(p)]
+        flipped[p, :, :unit] = value.T
+        for side in range(2):
+            if cuts(p, side):
+                @pl.when(core == side)
+                def _():
+                    for _, copy in flips(p, side):
+                        copy.start()
+        last[p] = total[theirs, columns(p)]
+        ends(p).start()
+        at = pl.ds(pl.multiple_of(panel_of(p) * LANES, LANES), LANES)
+        window[:, at] = total[mine, columns(p)]
+
+    for p in range(parts):
+        with jax.named_scope(f"send{p}_0"):
+            send(p, 0)
+    for copy in pair:
+        copy.wait_send()
+    level = [0] * parts
+    for p in STEPS_AFTER + list(range(parts)) * 8:
+        if p >= parts or level[p] >= len(plan[p]):
+            continue
+        if level[p] == 0:
+            with jax.named_scope(f"fill{p}"):
+                fill(p)
+        with jax.named_scope(f"wait{p}_{level[p]}"):
+            wait(p, level[p])
+        if level[p] + 1 < len(plan[p]):
+            with jax.named_scope(f"send{p}_{level[p] + 1}"):
+                send(p, level[p] + 1)
+        with jax.named_scope(f"keep{p}_{level[p]}"):
+            keep(p, level[p])
+        with jax.named_scope(f"sent{p}_{level[p]}"):
+            for m, (at, *_) in enumerate(messages_of(plan[p])):
+                if at == level[p]:
+                    for copy in copies(p, m):
+                        copy.wait_send()
+        level[p] += 1
+        if level[p] == len(plan[p]):
+            with jax.named_scope(f"finish{p}"):
+                finish(p)
+
+    with jax.named_scope("ends"):
+        for p in range(parts):
+            ends(p).wait_recv()
+    for k in range(reach + 1):
+        n, a = k * unit // LANES, k * unit % LANES
+        value = window[:, columns(n)]
+        if a:
+            if a + unit > LANES:
+                value = jnp.where(lane >= a, value, window[:, columns(n + 1)])
+            value = pltpu.roll(value, LANES - a, 1)
+        around[k] = value
+    with jax.named_scope("flips"):
+      for side in range(2):
+        @pl.when(core == side)
+        def _():
+            for p in range(parts):
+                for origin in range(2):
+                    for half, copy in flips(p, origin):
+                        if half == side:
+                            copy.wait_recv()
+
+    with jax.named_scope("out"):
+      for n in range(panels):
+        value, c = None, n * LANES
+        while c < (n + 1) * LANES:
+            b, off = c // own_rows, c % own_rows
+            g, m = b // members, b % members
+            z, x, y = m // 2, m % 2, g // 2
+            w = 2 * ladder - 1 - y if x else y
+            s = w * line + (line - 1 - z if w % 2 else z)
+            piece = around[lax.rem(s - own + chips, chips)]
+            shift = (c - n * LANES - (g % 2 * own_rows + off)) % LANES
+            piece = pltpu.roll(piece, shift, 1) if shift else piece
+            value = piece if value is None else jnp.where(lane >= c - n * LANES, piece, value)
+            c += min(own_rows - off, (n + 1) * LANES - c)
+        out_ref[:, columns(n)] = value
+
+    with jax.named_scope("last"):
+     for p in range(parts):
+        ends(p).wait_send()
+        for side in range(2):
+            if cuts(p, side):
+                @pl.when(core == side)
+                def _():
+                    for _, copy in flips(p, side):
+                        copy.wait_send()
+
+
+def circle_call(groups, members, rows, screen, own_rows, width):
+    depth, basis = rows.shape
+    unit = 2 * own_rows
+    chips = groups * members // 2
+    parts = -(-(chips // 2 + 1) * unit // LANES) // 2
+    plan = circle_plan(groups, members, parts)
+    levels = max(len(messages_of(stages)) for stages in plan)
+    places = max(8, chips // 2)
+    pieces = 4
+    dma = pltpu.SemaphoreType.DMA
+    vmem = pl.BlockSpec(memory_space=pltpu.VMEM)
+    return pl.pallas_call(
+        functools.partial(circle_kernel, groups, members, plan, width),
+        out_shape=pltpu.VMEM((own_rows, basis), jnp.float32),
+        in_specs=[pl.BlockSpec(memory_space=pl.ANY), pl.BlockSpec(memory_space=pltpu.SMEM)],
+        out_specs=vmem,
+        scratch_shapes=[
+            pltpu.VMEM((depth, basis), jnp.bfloat16),
+            pltpu.VMEM((2 * depth, basis + LANES), jnp.bfloat16),
+            pltpu.VMEM((basis, 2 * depth), jnp.bfloat16),
+            pltpu.VMEM((basis, parts * LANES), jnp.float32),
+            pltpu.VMEM((parts, chips - 1, unit, LANES), jnp.int16),
+            pltpu.VMEM((parts, chips - 1, unit, LANES), jnp.int16),
+            pltpu.VMEM((parts, levels, places, LANES), jnp.float32),
+            pltpu.VMEM((parts, levels, places, LANES), jnp.float32),
+            pltpu.VMEM((parts, own_rows, LANES), jnp.float32),
+            pltpu.VMEM((own_rows, 2 * parts * LANES), jnp.float32),
+            pltpu.VMEM((parts, LANES, LANES), jnp.float32),
+            pltpu.VMEM((chips, own_rows, LANES), jnp.float32),
+            dma((pieces,)), dma((pieces,)), dma((pieces,)),
+            dma((parts, levels)), dma((parts, levels)),
+            dma((parts, levels)), dma((parts, levels)),
+            dma((parts,)), dma((parts,)),
+            dma((parts, 8)), dma((2 * parts, 8)),
+        ],
+        compiler_params=pltpu.CompilerParams(
+            collective_id=1, has_side_effects=True, vmem_limit_bytes=60 * 1024 * 1024
+        ),
+    )(rows, screen)
+
+
+def circle_fits(groups, members, own_rows, basis, depth, width):
+    unit = 2 * own_rows
+    chips = groups * members // 2
+    panels = -(-(chips // 2 + 1) * unit // LANES)
+    return (
+        groups >= 4 and members >= 4 and 64 < unit <= LANES and unit % 16 == 0
+        and basis % 256 == 0 and panels % 2 == 0 and depth % (4 * width) == 0
+    )
+
+
 def solution(mesh):
     groups, members = mesh.shape["grp"], mesh.shape["mem"]
 
@@ -286,6 +765,9 @@
             rows = jnp.pad(rows, ((0, 0), (0, 0), (0, own_rows - real_rows)))
             basis = devices * own_rows
             rows = rows.reshape(depth, basis)
+        width = occ_count // screen.shape[1]
+        if own_rows == real_rows and circle_fits(groups, members, own_rows, basis, depth, width):
+            return circle_call(groups, members, rows, screen, own_rows, width)
         half = basis // 2
         parts = half // LANES
         plan = plan_for(groups, members, parts)

time: 49.5 us -> 46.4 us (0.937)
  Pallas kernels: 48.6 us -> 45.5 us
    pallas_call x1, Pallas kernels: 48.6 us -> 45.5 us  [circle_call(): pl.pallas_call(functools.partial(circle_kernel, groups, members, plan, wi...]
where the time goes in v1:
time: 46.4 us; the launch traced here: 46.2 us
  Pallas kernels  45.5 us (98%)
  local copies, waits for them, and re-layouts  0.75 us (2%)
    pallas_call x1, Pallas kernels, circle_call(): pl.pallas_call(functools.partial(circle_kernel, groups, members, plan, wi...  45.5 us

profile of v1, /device:TPU:0, one launch (start us, length us, event | category | flops | bytes accessed | tf_op | source)
XLA Modules:
  0.0 46.2 jit_solution(8052731825773833979)
XLA Ops:
  0.0 45.5 %shard_map.28 = f32[56,1792]{1,0:T(8,128)S(1)} custom-call(bf16[576,1792]{1,0:T(8,128)(2,1)} %bitcast.1, s32[1,18]{1,0:T(1,128)} %screen_ref.1), custom_call_target="tpu_custom_call" | custom-call | tf_op jit(solution)/shard_map/pallas_call | solution.py:713
  45.5 0.8 %copy.4 = f32[56,1792]{1,0:T(8,128)} copy(f32[56,1792]{1,0:T(8,128)S(1)} %shard_map.28) | data formatting | bytes 802816

commit v2 on v1

--- a/solution.py
+++ b/solution.py
@@ -273,17 +273,27 @@
 
 NEAR, ROW = ("mem", 1), ("grp", 2)
 ORDERS = ["xyab", "ayxb", "yabx", "yxab"]
-STEPS_AFTER = [0, 0, 2, 1, 3, 2, 0, 1, 3, 2, 0, 1, 3, 2, 1, 3]
+STARTS = ["a2", "a3", "r1", "r0", "b1", "b2", "b3", "f0", "f1", "f2", "f3"]
+ROUNDS = [0, 1, 2, 3] + [0, 2, 1, 3] * 3
+CODE = 256.0
+BEGIN = 8
+SPARE = 16
 
 
 def circle_plan(groups, members, parts):
     far = [("mem", 2 << k) for k in range(bits_of(members) - 1)]
+    rows = [("grp", 2 << k) for k in range(bits_of(groups) - 1)]
     letters = {
         "x": [[NEAR]],
-        "y": [[("grp", 2 << k)] for k in range(bits_of(groups) - 1)],
+        "y": [[bit] for bit in rows],
         "a": [far[:1]],
         "b": [[bit] for bit in far[1:]],
         "z": [far[::-1]],
+        "d": [rows + [NEAR]],
+        "e": [[NEAR] + far[:1]],
+        "f": [rows + far[:1]],
+        "g": [rows + far[1:]],
+        "h": [[NEAR] + far[1:]],
     }
     orders = [ORDERS[p % len(ORDERS)] for p in range(parts)]
     return [[stage for letter in order for stage in letters[letter]] for order in orders]
@@ -314,9 +324,8 @@
 
 def circle_kernel(
     groups, members, plan, width, x_hbm, screen_ref, out_ref,
-    x_ref, both, turned, total, sent, got, sent_top, got_top, last, window, flipped, around,
-    load, pair_send, pair_recv, data_send, data_recv, top_send, top_recv, end_send, end_recv,
-    flip_send, flip_recv,
+    x_ref, both, turned, raw, total, sent, got, sent_top, got_top, last, window, flipped, mirror, around,
+    load, pair_send, pair_recv, data_send, data_recv, end_send, end_recv, flip_send, flip_recv,
 ):
     depth, basis = x_ref.shape
     own_rows = out_ref.shape[0]
@@ -326,11 +335,12 @@
     for n in range(pieces):
         at = pl.ds(n * piece, piece)
         loads.append(pltpu.make_async_copy(x_hbm.at[at], x_ref.at[at], load.at[n]))
-        loads[-1].start()
+    loads[0].start()
     unit = 2 * own_rows
     chips = groups * members // 2
     line, ladder = members // 2, groups // 2
     reach = chips // 2
+    tall = (own_rows + 15) // 16 * 16
     parts = len(plan)
     panels = basis // LANES
     occ_blocks = screen_ref.shape[1]
@@ -386,6 +396,8 @@
     peers = [partner] + [peer(bits) for bits in sorted(met)]
     for other in peers:
         pl.semaphore_signal(barrier, inc=1, device_id=other, device_id_type=MESH)
+    for copy in loads[1:]:
+        copy.start()
 
     moves = moves_of(groups, members, own_rows, basis)
 
@@ -402,14 +414,14 @@
                     value = piece if value is None else jnp.where(lane >= first, piece, value)
                 value = value * keep
                 both[at, columns(n)] = value
-                if n == 0:
-                    both[at, columns(panels)] = value
+                if n < parts:
+                    both[at, columns(panels + n)] = value
         return carry
 
     def columns(p):
         return slice(p * LANES, (p + 1) * LANES)
 
-    strips = 3
+    strips = piece // width
     pair = []
     for n in range(pieces):
         with jax.named_scope(f"load{n}"):
@@ -422,8 +434,8 @@
                 pl.semaphore_wait(barrier, len(peers))
         pair.append(
             pltpu.make_async_remote_copy(
-                src_ref=both.at[pl.ds(n * piece, piece)],
-                dst_ref=both.at[pl.ds(depth + n * piece, piece)],
+                src_ref=both.at[pl.ds(n * piece, piece), 0:basis],
+                dst_ref=both.at[pl.ds(depth + n * piece, piece), 0:basis],
                 send_sem=pair_send.at[n], recv_sem=pair_recv.at[n],
                 device_id=partner, device_id_type=MESH,
             )
@@ -431,30 +443,11 @@
         pair[-1].start()
 
     def turn(low, high):
-        def one(m, carry):
-            at = pl.ds(pl.multiple_of(m * wide, LANES), wide)
-            for k in range(low, high, LANES):
-                turned[at, k : k + LANES] = both[k : k + LANES, at].T
-            return carry
-
-        wide = basis // 2
-        lax.fori_loop(0, 2, one, 0)
-
-    early = depth // LANES * LANES
-    with jax.named_scope("turn"):
-        turn(0, early)
-    done = 0
-    for low in range(early, 2 * depth, LANES):
-        while done < pieces and low + LANES > depth + done * piece:
-            with jax.named_scope(f"pair{done}"):
-                pair[done].wait_recv()
-            done += 1
-        with jax.named_scope(f"turn{low}"):
-            turn(low, low + LANES)
+        for k in range(low, high, LANES):
+            turned[:, k : k + LANES] = both[k : k + LANES, 0:basis].T
 
     def rows_of(stages, index):
         order = [bit for bits in stages for bit in bits]
-        flips = [b for t, b in enumerate(order) if False]
         there = dict(place)
         for t, bit in enumerate(order):
             flip = index // (1 << (len(order) - 1 - t)) % 2
@@ -486,64 +479,124 @@
     def block_at(s):
         return pl.ds(pl.multiple_of(s * unit, 16), unit)
 
+    def start_of(s):
+        start = s * unit + core * (parts * LANES)
+        return jnp.where(start >= basis, start - basis, start)
+
+    def multiply(s, low, high):
+        at = pl.ds(pl.multiple_of(start_of(s) // LANES * LANES, LANES), (parts + 1) * LANES)
+        value = jnp.dot(
+            turned[block_at(s), low:high], both[low:high, at], preferred_element_type=jnp.float32
+        )
+        raw[block_at(s), :] = raw[block_at(s), :] + value if low else value
+
     def product(p, s):
-        start = s * unit + panel_of(p) * LANES
-        start = jnp.where(start >= basis, start - basis, start)
-        n = start // LANES
-        a = start - n * LANES
-        value = jnp.dot(
-            turned[block_at(s), :],
-            both[:, pl.ds(pl.multiple_of(n * LANES, LANES), 2 * LANES)],
-            preferred_element_type=jnp.float32,
-        )
-        value = jnp.where(lane >= a, value[:, :LANES], value[:, LANES:])
+        a = lax.rem(start_of(s), LANES)
+        r = jnp.where(core == 0, parts - 1 - p, p)
+        left = raw[block_at(s), pl.ds(pl.multiple_of(r * LANES, LANES), LANES)]
+        right = raw[block_at(s), pl.ds(pl.multiple_of((r + 1) * LANES, LANES), LANES)]
+        value = jnp.where(lane >= a, left, right)
         return pltpu.roll(value, jnp.where(a == 0, 0, LANES - a), 1)
 
     def current(p, index):
         return total[block_at(rows_of(plan[p], index)), columns(p)]
 
+    def row_of(p, m):
+        return messages_of(plan[p])[m][4] * unit + m * SPARE
+
+    def block_of(p, m, index):
+        return pl.ds(pl.multiple_of(row_of(p, m) + index * unit, 16), unit)
+
     def arrived(p, level, index):
         value = None
-        for m, (at, _, _, _, slot) in enumerate(messages_of(plan[p])):
+        for m, (at, *_) in enumerate(messages_of(plan[p])):
             if at == level:
                 top = got_top[p, m, pl.ds(index, 1), :] * (1.0 / TOP)
-                one = got[p, slot + index].astype(jnp.int32).astype(jnp.float32) * top
+                one = got[p, block_of(p, m, index), :].astype(jnp.int32).astype(jnp.float32) * top
                 value = one if value is None else value + one
         return value
 
-    def copies(p, m):
-        level, target, _, count, slot = messages_of(plan[p])[m]
-        run = pl.ds(slot, count)
-        to = peer(chosen(plan[p][level], target))
-        return [
-            pltpu.make_async_remote_copy(
-                src_ref=here, dst_ref=there, send_sem=a.at[p, m], recv_sem=b.at[p, m],
-                device_id=to, device_id_type=MESH,
-            )
-            for here, there, a, b in (
-                (sent.at[p, run], got.at[p, run], data_send, data_recv),
-                (sent_top.at[p, m], got_top.at[p, m], top_send, top_recv),
-            )
-        ]
+    def copy_to(p, m, here, there):
+        level, target, *_ = messages_of(plan[p])[m]
+        pltpu.make_async_remote_copy(
+            src_ref=here, dst_ref=there, send_sem=data_send.at[p], recv_sem=data_recv.at[p, m],
+            device_id=peer(chosen(plan[p][level], target)), device_id_type=MESH,
+        ).start()
+
+    def start_run(p, m, low, high):
+        run = pl.ds(row_of(p, m) + low * unit, (high - low) * unit)
+        copy_to(p, m, sent.at[p, run], got.at[p, run])
+
+    def start_top(p, m):
+        copy_to(p, m, sent_top.at[p, m], got_top.at[p, m])
+
+    def crossing(p, index, bit=NEAR):
+        order = [b for bits in plan[p] for b in bits]
+        return index >> (len(order) - 1 - order.index(bit)) & 1
+
+    def whole(p, m):
+        count = messages_of(plan[p])[m][3]
+        run = pl.ds(row_of(p, m), count * unit + SPARE)
+        return pltpu.make_async_remote_copy(
+            src_ref=sent.at[p, run], dst_ref=got.at[p, run],
+            send_sem=data_send.at[p], recv_sem=data_recv.at[p, m],
+            device_id=partner, device_id_type=MESH,
+        )
+
+    def all_sent(p):
+        rows = row_of(p, 0) + (chips - 1) * unit + len(messages_of(plan[p])) * SPARE
+        pltpu.make_async_remote_copy(
+            src_ref=sent.at[p, pl.ds(0, rows)], dst_ref=got.at[p, pl.ds(0, rows)],
+            send_sem=data_send.at[p], recv_sem=data_recv.at[p, 0],
+            device_id=partner, device_id_type=MESH,
+        ).wait_send()
+
+    def multiply_all(first, last, low, high):
+        def one(t, carry):
+            for u in range(4):
+                multiply(rows_of(plan[0], first + t * 4 + u), low, high)
+            return carry
+
+        lax.fori_loop(0, (last - first) // 4, one, 0)
+
+    def pack(p, m, i):
+        level, _, first, _, _ = messages_of(plan[p])[m]
+        if level:
+            value = current(p, first + i) + arrived(p, level - 1, first + i)
+        else:
+            value = product(p, rows_of(plan[p], first + i))
+        top = jnp.max(jnp.abs(value), axis=0, keepdims=True)
+        scale = TOP / jnp.maximum(top, 2e-34)
+        packed = jnp.round(value * scale).astype(jnp.int32).astype(jnp.int16)
+        sent[p, block_of(p, m, i), :] = packed
+        sent_top[p, m, pl.ds(i, 1), :] = top
 
     def send(p, level):
-        for m, (at, _, first, count, slot) in reversed(list(enumerate(messages_of(plan[p])))):
-            if at != level:
+        for m, (at, _, _, count, _) in reversed(list(enumerate(messages_of(plan[p])))):
+            if at == level:
+                repeat(0, count, functools.partial(pack, p, m))
+                start_run(p, m, 0, count)
+                start_top(p, m)
+
+    def send_first(p, group, low=0, high=None):
+        for m, (at, _, first, count, _) in enumerate(messages_of(plan[p])):
+            if at:
                 continue
-
-            def pack(i):
-                if level:
-                    value = current(p, first + i) + arrived(p, level - 1, first + i)
+            chunk = [i for i in range(count) if crossing(p, first + i) == 1 - group]
+            ends_here = group == 1 or len(chunk) == count
+            chunk = chunk[low:high]
+            for i in chunk:
+                pack(p, m, i)
+            runs = []
+            for i in chunk:
+                if runs and runs[-1][1] == i:
+                    runs[-1][1] = i + 1
                 else:
-                    value = product(p, rows_of(plan[p], first + i))
-                top = jnp.max(jnp.abs(value), axis=0, keepdims=True)
-                scale = TOP / jnp.maximum(top, 2e-34)
-                sent[p, slot + i] = jnp.round(value * scale).astype(jnp.int32).astype(jnp.int16)
-                sent_top[p, m, pl.ds(i, 1), :] = top
-
-            repeat(0, count, pack)
-            for copy in copies(p, m):
-                copy.start()
+                    runs.append([i, i + 1])
+            for run in runs:
+                start_run(p, m, *run)
+            if chunk and ends_here and (high is None or high >= count):
+                start_top(p, m)
 
     def remaining(p, level):
         count = [n for at, _, _, n, _ in messages_of(plan[p]) if at == level][0]
@@ -559,8 +612,7 @@
     def wait(p, level):
         for m, (at, *_) in enumerate(messages_of(plan[p])):
             if at == level:
-                for copy in copies(p, m):
-                    copy.wait_recv()
+                whole(p, m).wait_recv()
 
     def keep(p, level):
         count = remaining(p, level)
@@ -574,66 +626,121 @@
 
     def cuts(p, side):
         q = parts - 1 - p if side == 0 else parts + p
-        marks = sorted({q * LANES, (q + 1) * LANES} | {
-            r for r in range(q * LANES, (q + 1) * LANES) if r % own_rows == 0
-        })
         result = []
-        for t, (low, high) in enumerate(zip(marks, marks[1:])):
-            k, half = low // unit, low % unit // own_rows
-            if 0 < k < reach:
-                result.append((q, t, k, half, low - q * LANES, low % own_rows, high - low))
+        for k in range(1, reach):
+            for half in range(2):
+                base = k * unit + (unit - tall) * half
+                low, high = max(base, q * LANES), min(base + tall, (q + 1) * LANES)
+                if low < high:
+                    result.append((k, half, low - q * LANES, low - base, high - low))
         return result
 
     def flips(p, side):
-        result = []
-        for q, t, k, half, here, there, count in cuts(p, side):
+        for k, half, here, there, count in cuts(p, side):
             g, m = holder(lax.rem(own + k, chips))
-            copy = pltpu.make_async_remote_copy(
-                src_ref=flipped.at[p, pl.ds(here, count)],
-                dst_ref=around.at[chips - k, pl.ds(there, count)],
-                send_sem=flip_send.at[p, t], recv_sem=flip_recv.at[q, t],
+            yield pltpu.make_async_remote_copy(
+                src_ref=flipped.at[pl.ds(p * LANES + here, count)],
+                dst_ref=mirror.at[pl.ds((k - 1) * tall + there, count)],
+                send_sem=flip_send, recv_sem=flip_recv,
                 device_id=(g + half, m), device_id_type=MESH,
             )
-            result.append((half, copy))
-        return result
+
+    def flips_like(ref, count):
+        run = pl.ds(0, count)
+        return pltpu.make_async_remote_copy(
+            src_ref=ref.at[run], dst_ref=ref.at[run], send_sem=flip_send, recv_sem=flip_recv,
+            device_id=partner, device_id_type=MESH,
+        )
 
     def ends(p):
         q = panel_of(p)
         at = pl.ds(pl.multiple_of(q * LANES, LANES), LANES)
         return pltpu.make_async_remote_copy(
             src_ref=last.at[p], dst_ref=window.at[:, at],
-            send_sem=end_send.at[p], recv_sem=end_recv.at[p],
+            send_sem=end_send, recv_sem=end_recv,
+            device_id=partner, device_id_type=MESH,
+        )
+
+    def all_ends():
+        at = pl.ds(pl.multiple_of((1 - core) * parts * LANES, LANES), parts * LANES)
+        return pltpu.make_async_remote_copy(
+            src_ref=window.at[:, at], dst_ref=window.at[:, at],
+            send_sem=end_send, recv_sem=end_recv,
             device_id=partner, device_id_type=MESH,
         )
 
     def finish(p):
         mine = pl.ds(pl.multiple_of(own * unit + core * own_rows, 8), own_rows)
         theirs = pl.ds(pl.multiple_of(own * unit + (1 - core) * own_rows, 8), own_rows)
-        value = total[block_at(own), columns(p)]
-        flipped[p, :, :unit] = value.T
+        last[p] = total[theirs, columns(p)]
+        ends(p).start()
+        if cuts(p, 0) or cuts(p, 1):
+            value = total[block_at(own), columns(p)]
+            top = jnp.max(jnp.abs(value), axis=0, keepdims=True)
+            code = jnp.ceil(jnp.log2(jnp.maximum(top, 2e-34)) * CODE) + 1.0
+            scale = TOP * jnp.exp2(code * (-1.0 / CODE))
+            code = jnp.broadcast_to(code, (LANES - unit, LANES))
+            value = jnp.concatenate([jnp.round(value * scale), code], axis=0).T
+            flipped[p * LANES : (p + 1) * LANES, :] = value.astype(jnp.int32).astype(jnp.int16)
         for side in range(2):
             if cuts(p, side):
                 @pl.when(core == side)
                 def _():
-                    for _, copy in flips(p, side):
+                    for copy in flips(p, side):
                         copy.start()
-        last[p] = total[theirs, columns(p)]
-        ends(p).start()
         at = pl.ds(pl.multiple_of(panel_of(p) * LANES, LANES), LANES)
         window[:, at] = total[mine, columns(p)]
 
-    for p in range(parts):
-        with jax.named_scope(f"send{p}_0"):
-            send(p, 0)
-    for copy in pair:
-        copy.wait_send()
+    early = depth // LANES * LANES
+    with jax.named_scope("turn"):
+        turn(0, early)
+    later = chips - BEGIN
+    with jax.named_scope("begin"):
+        multiply_all(later, chips, 0, early)
+    done = 0
+    for low in range(early, 2 * depth, LANES):
+        while done < pieces and low + LANES > depth + done * piece:
+            with jax.named_scope(f"pair{done}"):
+                pair[done].wait_recv()
+            done += 1
+        with jax.named_scope(f"turn{low}"):
+            if low + LANES > depth:
+                rows = slice(max(low, depth), low + LANES)
+                both[rows, basis:] = both[rows, : parts * LANES]
+            turn(low, low + LANES)
+    half = (chips + later) // 2
+    with jax.named_scope("multiply"):
+        multiply_all(later, half, early, 2 * depth)
+    with jax.named_scope("send0_0"):
+        send_first(0, 0, 0, half - later)
+    with jax.named_scope("multiply2"):
+        multiply_all(half, chips, early, 2 * depth)
+    with jax.named_scope("send1_0a"):
+        send_first(1, 0)
+    with jax.named_scope("send0_0b"):
+        send_first(0, 0, half - later, chips)
     level = [0] * parts
-    for p in STEPS_AFTER + list(range(parts)) * 8:
+    filled = [False] * parts
+    for word in STARTS + [str(p) for p in ROUNDS + list(range(parts)) * 8]:
+        if word[0] == "r":
+            with jax.named_scope("rest" + word[1]):
+                for i in range(later):
+                    if crossing(0, i, ("mem", 2)) == int(word[1]):
+                        multiply(rows_of(plan[0], i), 0, 2 * depth)
+            continue
+        p = int(word[-1])
         if p >= parts or level[p] >= len(plan[p]):
             continue
-        if level[p] == 0:
+        if word[0] in "ab":
+            with jax.named_scope(f"send{word}"):
+                send_first(p, "ab".index(word[0]))
+            continue
+        if not filled[p]:
             with jax.named_scope(f"fill{p}"):
                 fill(p)
+            filled[p] = True
+        if word[0] == "f":
+            continue
         with jax.named_scope(f"wait{p}_{level[p]}"):
             wait(p, level[p])
         if level[p] + 1 < len(plan[p]):
@@ -641,19 +748,13 @@
                 send(p, level[p] + 1)
         with jax.named_scope(f"keep{p}_{level[p]}"):
             keep(p, level[p])
-        with jax.named_scope(f"sent{p}_{level[p]}"):
-            for m, (at, *_) in enumerate(messages_of(plan[p])):
-                if at == level[p]:
-                    for copy in copies(p, m):
-                        copy.wait_send()
         level[p] += 1
         if level[p] == len(plan[p]):
             with jax.named_scope(f"finish{p}"):
                 finish(p)
 
     with jax.named_scope("ends"):
-        for p in range(parts):
-            ends(p).wait_recv()
+        all_ends().wait_recv()
     for k in range(reach + 1):
         n, a = k * unit // LANES, k * unit % LANES
         value = window[:, columns(n)]
@@ -663,40 +764,35 @@
             value = pltpu.roll(value, LANES - a, 1)
         around[k] = value
     with jax.named_scope("flips"):
-      for side in range(2):
-        @pl.when(core == side)
-        def _():
-            for p in range(parts):
-                for origin in range(2):
-                    for half, copy in flips(p, origin):
-                        if half == side:
-                            copy.wait_recv()
-
+        flips_like(mirror, (reach - 1) * tall).wait_recv()
+    for k in range(1, reach):
+        low = (k - 1) * tall
+        value = mirror[low : low + tall, :].astype(jnp.int32).astype(jnp.float32)
+        value = jnp.where(core == 0, value[:own_rows], value[tall - own_rows :])
+        scale = jnp.exp2(value[:, unit : unit + 1] * (1.0 / CODE)) * (1.0 / TOP)
+        around[chips - k] = value * scale
     with jax.named_scope("out"):
       for n in range(panels):
         value, c = None, n * LANES
         while c < (n + 1) * LANES:
             b, off = c // own_rows, c % own_rows
             g, m = b // members, b % members
-            z, x, y = m // 2, m % 2, g // 2
-            w = 2 * ladder - 1 - y if x else y
-            s = w * line + (line - 1 - z if w % 2 else z)
+            s = next(s for s in range(chips) if place_of(groups, members, s) == (g // 2, m // 2, m % 2))
             piece = around[lax.rem(s - own + chips, chips)]
             shift = (c - n * LANES - (g % 2 * own_rows + off)) % LANES
             piece = pltpu.roll(piece, shift, 1) if shift else piece
             value = piece if value is None else jnp.where(lane >= c - n * LANES, piece, value)
             c += min(own_rows - off, (n + 1) * LANES - c)
         out_ref[:, columns(n)] = value
-
-    with jax.named_scope("last"):
-     for p in range(parts):
-        ends(p).wait_send()
+    with jax.named_scope("sents"):
+        for copy in pair:
+            copy.wait_send()
+        for p in range(parts):
+            all_sent(p)
         for side in range(2):
-            if cuts(p, side):
-                @pl.when(core == side)
-                def _():
-                    for _, copy in flips(p, side):
-                        copy.wait_send()
+            count = sum(cut[4] for p in range(parts) for cut in cuts(p, side))
+            pl.when(core == side)(flips_like(flipped, count).wait_send)
+        all_ends().wait_send()
 
 
 def circle_call(groups, members, rows, screen, own_rows, width):
@@ -706,7 +802,9 @@
     parts = -(-(chips // 2 + 1) * unit // LANES) // 2
     plan = circle_plan(groups, members, parts)
     levels = max(len(messages_of(stages)) for stages in plan)
-    places = max(8, chips // 2)
+    places = SPARE // 2
+    deep = (chips - 1) * unit + levels * SPARE
+    tall = (own_rows + 15) // 16 * 16
     pieces = 4
     dma = pltpu.SemaphoreType.DMA
     vmem = pl.BlockSpec(memory_space=pltpu.VMEM)
@@ -717,22 +815,21 @@
         out_specs=vmem,
         scratch_shapes=[
             pltpu.VMEM((depth, basis), jnp.bfloat16),
-            pltpu.VMEM((2 * depth, basis + LANES), jnp.bfloat16),
+            pltpu.VMEM((2 * depth, basis + parts * LANES), jnp.bfloat16),
             pltpu.VMEM((basis, 2 * depth), jnp.bfloat16),
+            pltpu.VMEM((basis, (parts + 1) * LANES), jnp.float32),
             pltpu.VMEM((basis, parts * LANES), jnp.float32),
-            pltpu.VMEM((parts, chips - 1, unit, LANES), jnp.int16),
-            pltpu.VMEM((parts, chips - 1, unit, LANES), jnp.int16),
+            pltpu.VMEM((parts, deep, LANES), jnp.int16),
+            pltpu.VMEM((parts, deep, LANES), jnp.int16),
             pltpu.VMEM((parts, levels, places, LANES), jnp.float32),
             pltpu.VMEM((parts, levels, places, LANES), jnp.float32),
             pltpu.VMEM((parts, own_rows, LANES), jnp.float32),
             pltpu.VMEM((own_rows, 2 * parts * LANES), jnp.float32),
-            pltpu.VMEM((parts, LANES, LANES), jnp.float32),
+            pltpu.VMEM((parts * LANES, LANES), jnp.int16),
+            pltpu.VMEM(((chips // 2 - 1) * tall, LANES), jnp.int16),
             pltpu.VMEM((chips, own_rows, LANES), jnp.float32),
             dma((pieces,)), dma((pieces,)), dma((pieces,)),
-            dma((parts, levels)), dma((parts, levels)),
-            dma((parts, levels)), dma((parts, levels)),
-            dma((parts,)), dma((parts,)),
-            dma((parts, 8)), dma((2 * parts, 8)),
+            dma((parts,)), dma((parts, levels)), dma, dma, dma, dma,
         ],
         compiler_params=pltpu.CompilerParams(
             collective_id=1, has_side_effects=True, vmem_limit_bytes=60 * 1024 * 1024
@@ -745,7 +842,8 @@
     chips = groups * members // 2
     panels = -(-(chips // 2 + 1) * unit // LANES)
     return (
-        groups >= 4 and members >= 4 and 64 < unit <= LANES and unit % 16 == 0
+        groups >= 4 and members >= 4 and 64 < unit < LANES and unit % 16 == 0
+        and chips // 2 <= SPARE // 2
         and basis % 256 == 0 and panels % 2 == 0 and depth % (4 * width) == 0
     )
 

time: 46.4 us -> 37.9 us (0.82)
  Pallas kernels: 45.5 us -> 36.9 us
    pallas_call x1, Pallas kernels: 45.5 us -> 36.9 us  [circle_call(): pl.pallas_call(functools.partial(circle_kernel, groups, members, plan, wi...]
where the time goes in v2:
time: 37.9 us; the launch traced here: 37.7 us
  Pallas kernels  36.9 us (97%)
  local copies, waits for them, and re-layouts  0.75 us (2%)
    pallas_call x1, Pallas kernels, circle_call(): pl.pallas_call(functools.partial(circle_kernel, groups, members, plan, wi...  36.9 us

profile of v2, /device:TPU:0, one launch (start us, length us, event | category | flops | bytes accessed | tf_op | source)
XLA Modules:
  0.0 37.7 jit_solution(5923992881263996979)
XLA Ops:
  0.0 36.9 %shard_map.28 = f32[56,1792]{1,0:T(8,128)S(1)} custom-call(bf16[576,1792]{1,0:T(8,128)(2,1)} %bitcast.1, s32[1,18]{1,0:T(1,128)} %screen_ref.1), custom_call_target="tpu_custom_call" | custom-call | tf_op jit(solution)/shard_map/pallas_call | solution.py:811
  37.0 0.8 %copy.4 = f32[56,1792]{1,0:T(8,128)} copy(f32[56,1792]{1,0:T(8,128)S(1)} %shard_map.28) | data formatting | bytes 802816

commit v3 on v2

--- a/solution.py
+++ b/solution.py
@@ -278,6 +278,7 @@
 CODE = 256.0
 BEGIN = 8
 SPARE = 16
+PIECES = 6
 
 
 def circle_plan(groups, members, parts):
@@ -805,7 +806,7 @@
     places = SPARE // 2
     deep = (chips - 1) * unit + levels * SPARE
     tall = (own_rows + 15) // 16 * 16
-    pieces = 4
+    pieces = PIECES
     dma = pltpu.SemaphoreType.DMA
     vmem = pl.BlockSpec(memory_space=pltpu.VMEM)
     return pl.pallas_call(
@@ -844,7 +845,7 @@
     return (
         groups >= 4 and members >= 4 and 64 < unit < LANES and unit % 16 == 0
         and chips // 2 <= SPARE // 2
-        and basis % 256 == 0 and panels % 2 == 0 and depth % (4 * width) == 0
+        and basis % 256 == 0 and panels % 2 == 0 and depth % (PIECES * width) == 0
     )
 
 

time: 37.9 us -> 39.2 us (1.034)
  Pallas kernels: 36.9 us -> 38.3 us
    pallas_call x1, Pallas kernels: 36.9 us -> 38.3 us  [circle_call(): pl.pallas_call(functools.partial(circle_kernel, groups, members, plan, wi...]
where the time goes in v3:
time: 39.2 us; the launch traced here: 39.1 us
  Pallas kernels  38.3 us (98%)
  local copies, waits for them, and re-layouts  0.75 us (2%)
    pallas_call x1, Pallas kernels, circle_call(): pl.pallas_call(functools.partial(circle_kernel, groups, members, plan, wi...  38.3 us

profile of v3, /device:TPU:0, one launch (start us, length us, event | category | flops | bytes accessed | tf_op | source)
XLA Modules:
  0.0 39.1 jit_solution(3151953066727717518)
XLA Ops:
  0.0 38.3 %shard_map.28 = f32[56,1792]{1,0:T(8,128)S(1)} custom-call(bf16[576,1792]{1,0:T(8,128)(2,1)} %bitcast.1, s32[1,18]{1,0:T(1,128)} %screen_ref.1), custom_call_target="tpu_custom_call" | custom-call | tf_op jit(solution)/shard_map/pallas_call | solution.py:812
  38.3 0.8 %copy.4 = f32[56,1792]{1,0:T(8,128)} copy(f32[56,1792]{1,0:T(8,128)S(1)} %shard_map.28) | data formatting | bytes 802816
